TPU v7x, 256 devices: a whole 4x4x8 slice. The times are simulated.
256 devices in a mesh: freq: 8 (over z_lo, x), panel: 32 (over z_hi, y, core).
Axes of the slice: x: 4, y: 4, z: 8 (z_hi: 4, z_lo: 2; z = z_hi * 2 + z_lo), core: 2. Of those that a mesh axis runs over, the one named last changes fastest.
Arguments:
- recorded: float32 [8, 2, 2048, 2048], P('freq', None, 'panel'), parts along dimension 0, may hold values from -60 to 60
- receiver_kernel: bfloat16 [8, 2, 4095], P('freq'), parts along dimension 0, may hold values from -1.5 to 1.5
- source_kernel: bfloat16 [8, 2, 4095], P('freq'), parts along dimension 0, may hold values from -1.5 to 1.5
Outputs:
- primaries: float32 [8, 2, 2048, 2048], P('freq', None, 'panel'), parts along dimension 0
- multiples: bfloat16 [8, 2, 2048, 2048], P('freq', None, 'panel'), parts along dimension 0
There are 8 independent parts, one for each index of `freq`. A program takes and returns all parts, laid end to end along the dimension named above; each array names one. Nothing has to cross between parts.
All inputs are finite; a program needn't handle non-finite values.
Results may differ from a plain program's by a relative error of at most 0.0057.
Values may be sent and summed in bfloat16 or wider, within the bound.
A program may use at most 320 MiB of HBM per device.

v0:
```python
import jax
import jax.numpy as jnp
from jax import lax
from jax.sharding import PartitionSpec as P


def from_everyone(value, axis):
    copies = jnp.broadcast_to(value, (lax.axis_size(axis), *value.shape))
    return lax.all_to_all(copies, axis, split_axis=0, concat_axis=0, tiled=True)


def over_copies(value, axis):
    everything = from_everyone(value, axis)
    return jnp.sum(everything, axis=0)


def packed_total(arrays, axis):
    flat, at, outs = (jnp.concatenate([a.reshape(-1) for a in arrays]), 0, [])
    running = over_copies(flat, axis)
    for a in arrays:
        outs.append(running[at : at + a.size].reshape(a.shape))
        at += a.size
    return tuple(outs)


def band(kernel, base, nrows, ncols):
    length = nrows + ncols - 1
    piece = lax.dynamic_slice_in_dim(kernel, base - nrows + 1, length, 1)
    rolled = jnp.roll(piece, -(nrows - 1), axis=1)
    flat = jnp.tile(rolled, (1, nrows))[:, : nrows * (length - 1)]
    return flat.reshape(2, nrows, length - 1)[:, :, :ncols]


def complex_dot(left, right):
    real_part = jnp.dot(left[0], right[0], preferred_element_type=jnp.float32) - jnp.dot(
        left[1], right[1], preferred_element_type=jnp.float32
    )
    imag_part = jnp.dot(left[0], right[1], preferred_element_type=jnp.float32) + jnp.dot(
        left[1], right[0], preferred_element_type=jnp.float32
    )
    return jnp.stack([real_part, imag_part])


def per_device(recorded, receiver_kernel, source_kernel):
    freqs, rows, width = (recorded.shape[0], recorded.shape[2], recorded.shape[3])
    panels = lax.axis_size("panel")
    sources = rows * panels
    data_b = recorded.astype(jnp.bfloat16)
    focused = jnp.stack(
        [complex_dot(data_b[0], band(receiver_kernel[0], width - 1, width, width))]
    ).astype(jnp.bfloat16)
    row_first = lax.axis_index("panel") * rows
    local_oper = jnp.stack([band(source_kernel[0], sources - 1 - row_first, rows, sources)])
    oper = local_oper[0]
    parts = [complex_dot(oper, lax.all_gather(focused, "panel", axis=2, tiled=True)[0])]
    summed = jnp.stack(parts)
    mult = summed.astype(jnp.bfloat16)
    mfl = mult.astype(jnp.float32)
    num_re = jnp.sum(mfl[:, 0] * recorded[:, 0] + mfl[:, 1] * recorded[:, 1], axis=(1, 2))
    num_im = jnp.sum(mfl[:, 0] * recorded[:, 1] - mfl[:, 1] * recorded[:, 0], axis=(1, 2))
    energy = jnp.sum(mfl[:, 0] * mfl[:, 0] + mfl[:, 1] * mfl[:, 1], axis=(1, 2))
    num_re, num_im, energy = packed_total((num_re, num_im, energy), "panel")
    den = energy + 1e-06
    fit_re = (num_re / den)[:, None, None]
    fit_im = (num_im / den)[:, None, None]
    prim_re = recorded[:, 0] - (fit_re * mfl[:, 0] - fit_im * mfl[:, 1])
    prim_im = recorded[:, 1] - (fit_re * mfl[:, 1] + fit_im * mfl[:, 0])
    return (jnp.stack([prim_re, prim_im], axis=1), mult)


def solution(mesh):
    placed = (P("freq", None, "panel", None), P("freq", None, None), P("freq", None, None))
    return jax.shard_map(
        per_device,
        mesh=mesh,
        in_specs=placed,
        out_specs=(P("freq", None, "panel", None), P("freq", None, "panel", None)),
        check_vma=False,
    )
```

profile of v0, /device:TPU:1, one launch (start us, length us, event | category | flops | bytes accessed | tf_op | source)
XLA Modules:
  0.0 450.9 jit_solution(5513023352090350222)
XLA Ops:
  7.2 0.0 copy-start
  7.2 0.0 all-gather.2.cloned.1.call-start
  7.2 0.8 slice.125
  8.0 0.7 slice.126
  8.7 11.1 %tile.20 = bf16[2,2048,4095]{2,1,0:T(8,128)(2,1)} broadcast(bf16[2,4095]{1,0:T(2,128)(2,1)S(1)} %pad_maximum_fusion.3), dimensions={0,2} | broadcast | bytes 33562620 | tf_op jit(solution)/shard_map/tile | solution.py:30
  19.8 69.4 %reshape.275 = bf16[16773120]{0:T(1024)(128)(2,1)} reshape(bf16[2,2048,4095]{2,1,0:T(8,128)(2,1)} %tile.20) | data formatting | bytes 67092480
  89.2 39.9 %tile.21 = bf16[2,8386560]{1,0:T(2,128)(2,1)} reshape(bf16[16773120]{0:T(1024)(128)(2,1)} %reshape.275) | data formatting | bytes 67092480 | tf_op jit(solution)/shard_map/tile | solution.py:30
  129.2 27.0 %slice.127 = bf16[2,8384512]{1,0:T(2,128)(2,1)} slice(bf16[2,8386560]{1,0:T(2,128)(2,1)} %tile.21), slice={[0:2], [0:8384512]} | slice | bytes 67076096 | tf_op jit(solution)/shard_map/slice | solution.py:30
  156.2 52.8 %reshape.277 = bf16[16769024]{0:T(1024)(128)(2,1)} reshape(bf16[2,8384512]{1,0:T(2,128)(2,1)} %slice.127) | data formatting | bytes 67076096
  209.0 0.0 copy-start.1
  209.0 53.1 %reshape.274 = bf16[2,2048,4094]{2,1,0:T(8,128)(2,1)} reshape(bf16[16769024]{0:T(1024)(128)(2,1)} %reshape.277) | data formatting | bytes 67076096 | tf_op jit(solution)/shard_map/reshape | solution.py:31
  262.1 0.0 copy-done.1
  262.1 0.1 convert_element_type.36
  262.2 4.9 %fusion = f32[2048,64]{0,1:T(8,128)S(1)} fusion(bf16[2,2048,4094]{2,1,0:T(8,128)(2,1)} %reshape.274, bf16[1,2,64,2048]{3,2,1,0:T(8,128)(2,1)S(1)} %convert_element_type.36), kind=kOutput, calls=%fused_computation.4 | convolution fusion | flops 536870912 | bytes 9175040 | tf_op jit(solution)/shard_map/dot_general | solution.py:35
  267.1 4.9 %fusion.1 = f32[2048,64]{0,1:T(8,128)S(1)} fusion(bf16[2,2048,4094]{2,1,0:T(8,128)(2,1)} %reshape.274, bf16[1,2,64,2048]{3,2,1,0:T(8,128)(2,1)S(1)} %convert_element_type.36), kind=kOutput, calls=%fused_computation.5 | convolution fusion | flops 536870912 | bytes 9175040 | tf_op jit(solution)/shard_map/dot_general | solution.py:38
  272.1 5.0 %fusion.19 = bf16[1,1,64,2048]{3,2,1,0:T(8,128)(2,1)S(1)} fusion(f32[2048,64]{0,1:T(8,128)S(1)} %fusion, bf16[2,2048,4094]{2,1,0:T(8,128)(2,1)} %reshape.274, bf16[1,2,64,2048]{3,2,1,0:T(8,128)(2,1)S(1)} %convert_element_type.36), kind=kOutput, calls=%fused_computation.23 | convolution fusion | flops 537133056 | bytes 9437184 | tf_op jit(solution)/shard_map/dot_general | solution.py:35
  277.0 5.0 %fusion.18 = bf16[1,1,64,2048]{3,2,1,0:T(8,128)(2,1)S(1)} fusion(f32[2048,64]{0,1:T(8,128)S(1)} %fusion.1, bf16[2,2048,4094]{2,1,0:T(8,128)(2,1)} %reshape.274, bf16[1,2,64,2048]{3,2,1,0:T(8,128)(2,1)S(1)} %convert_element_type.36), kind=kOutput, calls=%fused_computation.22 | convolution fusion | flops 537133056 | bytes 9437184 | tf_op jit(solution)/shard_map/dot_general | solution.py:38
  282.0 0.8 pad_maximum_fusion.1
  282.8 0.0 all-gather.2.cloned.1.call-update
  282.8 0.0 copy-done
  282.9 0.1 dynamic-slice_bitcast_fusion
  282.9 0.1 slice.120
  283.1 0.9 tile.9
  284.0 0.6 slice.122
  284.7 1.5 reshape.273
  286.2 106.4 %all-gather.2.cloned.1.call-done = bf16[1,2,2048,2048]{3,2,1,0:T(8,128)(2,1)} async-done(((bf16[1,2,64,2048]{3,2,1,0:T(8,128)(2,1)}), bf16[1,2,2048,2048]{3,2,1,0:T(8,128)(2,1)}) %all-gather.2.cloned.1.call-update) | async-done | bytes 16777232 | tf_op jit(solution)/shard_map/all_gather | solution.py:55
  392.6 0.0 copy-start.2
  392.6 5.1 %fusion.5 = f32[64,2048]{1,0:T(8,128)S(1)} fusion(bf16[1,2,2048,2048]{3,2,1,0:T(8,128)(2,1)} %all-gather.2.cloned.1.call-done, bf16[2,64,2110]{2,1,0:T(8,128)(2,1)S(1)} %reshape.273), kind=kOutput, calls=%fused_computation.9 | convolution fusion | flops 536870912 | bytes 9175040 | tf_op jit(solution)/shard_map/dot_general | solution.py:35
  397.7 5.7 %fusion.4 = f32[64,2048]{1,0:T(8,128)S(1)} fusion(bf16[1,2,2048,2048]{3,2,1,0:T(8,128)(2,1)} %all-gather.2.cloned.1.call-done, bf16[2,64,2110]{2,1,0:T(8,128)(2,1)S(1)} %reshape.273), kind=kOutput, calls=%fused_computation.8 | convolution fusion | flops 536870912 | bytes 9175040 | tf_op jit(solution)/shard_map/dot_general | solution.py:38
  403.4 0.0 copy-done.2
  403.4 1.6 fusion.16
  405.0 1.6 fusion.17
  406.6 0.9 fusion.20
  407.4 0.9 add_reduce_fusion.1
  408.4 2.0 pad_maximum_fusion.5
  410.4 29.6 %all_to_all.6 = f32[32,1,3]{2,1,0:T(1,128)S(1)} all-to-all(f32[32,1,3]{2,1,0:T(1,128)S(1)} %broadcast_in_dim.2), channel_id=1, replica_groups=mesh['freq'=8,'panel'=32] {'panel'}, dimensions={0} | all-to-all | bytes 768 | tf_op jit(solution)/shard_map/all_to_all | solution.py:9
  440.0 0.1 reduce_sum.48
  440.0 0.7 fusion.21
  442.6 0.2 subtract_subtract_fusion
  442.8 1.0 pad_maximum_fusion
  (5 shorter events, 0.1 us)
Async XLA Ops:
  7.2 275.7 %copy-start = (bf16[1,2,4095]{2,1,0:T(2,128)(2,1)S(1)}, bf16[1,2,4095]{2,1,0:T(2,128)(2,1)}, u32[]{:S(2)}) copy-start(bf16[1,2,4095]{2,1,0:T(2,128)(2,1)} %param.5) | copy-start | bytes 49144
  7.2 385.4 %all-gather.2.cloned.1.call-start = ((), (), s32[]{:S(2)}) async-start(), calls=%async_computation.1 | async-start | bytes 17301504 | tf_op jit(solution)/shard_map/all_gather | solution.py:55
  209.0 53.1 %copy-start.1 = (f32[1,2,64,2048]{3,2,1,0:T(8,128)S(1)}, f32[1,2,64,2048]{3,2,1,0:T(8,128)}, u32[]{:S(2)}) copy-start(f32[1,2,64,2048]{3,2,1,0:T(8,128)} %param.3) | copy-start | bytes 3145732
  392.6 10.8 %copy-start.2 = (bf16[1,2,2048,2048]{3,2,1,0:T(8,128)(2,1)S(1)}, bf16[1,2,2048,2048]{3,2,1,0:T(8,128)(2,1)}, u32[]{:S(2)}) copy-start(bf16[1,2,2048,2048]{3,2,1,0:T(8,128)(2,1)} %all-gather.2.cloned.1.call-done) | copy-start | bytes 50331652
Sparse Core Ops, SparseCore 0:
  283.0 109.5 all-gather.1
where the time goes:
time: 459 us; the launch traced here: 451 us
  local copies, waits for them, and re-layouts  259 us (56%)
  waiting for transfers between devices  106 us (23%)
  matrix products  33.7 us (7%)
  blocking collectives  29.6 us (6%)
  between operations  16.3 us (4%)
  other arithmetic  6.01 us (1%)
    unnamed x8, local copies, waits for them, and re-layouts  122 us
    all_gather x1, waiting for transfers between devices, per_device(): lax.all_gather(focused, 'panel', axis=2, tiled=True)[0]  106 us
    reshape x2, local copies, waits for them, and re-layouts, band(): return flat.reshape(2, nrows, length - 1)[:, :, :ncols]  54.6 us
    another operation x4, local copies, waits for them, and re-layouts, band(): flat = jnp.tile(rolled, (1, nrows))[:, :nrows * (length - 1)]  52 us
    all_to_all x1, blocking collectives, from_everyone(): return lax.all_to_all(copies, axis, split_axis=0, concat_axis=0, tiled=True)  29.6 us
    slice x2, local copies, waits for them, and re-layouts, band(): flat = jnp.tile(rolled, (1, nrows))[:, :nrows * (length - 1)]  27.7 us
    dot_general x2, matrix products, complex_dot(): jnp.dot(left[1], right[0], preferred_element_type=jnp.float32)  10.6 us
    dot_general x2, matrix products, complex_dot(): jnp.dot(left[0], right[0], preferred_element_type=jnp.float32)  10 us
  transfers between devices with their start and end apart: 1, of which 1 were waited for; matrix products, arithmetic and copies ran while one was open for 1% of the time, Pallas kernels for 0%

commit v1 on v0

--- a/solution.py
+++ b/solution.py
@@ -52,7 +52,14 @@
     row_first = lax.axis_index("panel") * rows
     local_oper = jnp.stack([band(source_kernel[0], sources - 1 - row_first, rows, sources)])
     oper = local_oper[0]
-    parts = [complex_dot(oper, lax.all_gather(focused, "panel", axis=2, tiled=True)[0])]
+    parts = [
+        complex_dot(
+            oper,
+            jnp.concatenate(
+                lax.all_to_all(jnp.stack([focused] * lax.axis_size("panel")), "panel", 0, 0), axis=2
+            )[0],
+        )
+    ]
     summed = jnp.stack(parts)
     mult = summed.astype(jnp.bfloat16)
     mfl = mult.astype(jnp.float32)

time: 459 us -> 705 us (1.54)
  waiting for transfers between devices: 106 us -> 363 us
  blocking collectives: 29.6 us -> 14.9 us
  between operations: 16.3 us -> 2.97 us
  local copies, waits for them, and re-layouts: 259 us -> 272 us
  starting transfers between devices: 0.04 us -> 13 us
  matrix products: 33.7 us -> 26.3 us
    all_to_all x0 -> x1, waiting for transfers between devices: none -> 363 us  [per_device(): lax.all_to_all(jnp.stack([focused] * lax.axis_size('panel')), 'panel', 0, 0)]
    all_gather x1 -> x0, waiting for transfers between devices: 106 us -> none  [per_device(): lax.all_gather(focused, 'panel', axis=2, tiled=True)[0]]
    all_to_all x1, blocking collectives: 29.6 us -> 14.9 us  [from_everyone(): return lax.all_to_all(copies, axis, split_axis=0, concat_axis=0, tiled=True)]
    all_to_all x0 -> x1, starting transfers between devices: none -> 13 us  [per_device(): lax.all_to_all(jnp.stack([focused] * lax.axis_size('panel')), 'panel', 0, 0)]
    unnamed x8 -> x6, local copies, waits for them, and re-layouts: 122 us -> 122 us
  transfers between devices with their start and end apart: 1 -> 1, of which waited for: 1 -> 1; matrix products, arithmetic and copies ran while one was open for 1% -> 0% of each run, Pallas kernels for 0% -> 0%
where the time goes in v1:
time: 705 us; the launch traced here: 696 us
  waiting for transfers between devices  363 us (51%)
  local copies, waits for them, and re-layouts  272 us (39%)
  matrix products  26.3 us (4%)
  blocking collectives  14.9 us (2%)
  starting transfers between devices  13 us (2%)
    all_to_all x1, waiting for transfers between devices, per_device(): lax.all_to_all(jnp.stack([focused] * lax.axis_size('panel')), 'panel', 0, 0)  363 us
    unnamed x6, local copies, waits for them, and re-layouts  122 us
    reshape x2, local copies, waits for them, and re-layouts, band(): return flat.reshape(2, nrows, length - 1)[:, :, :ncols]  54.6 us
    another operation x4, local copies, waits for them, and re-layouts, band(): flat = jnp.tile(rolled, (1, nrows))[:, :nrows * (length - 1)]  52 us
    slice x2, local copies, waits for them, and re-layouts, band(): flat = jnp.tile(rolled, (1, nrows))[:, :nrows * (length - 1)]  27.4 us
    all_to_all x1, blocking collectives, from_everyone(): return lax.all_to_all(copies, axis, split_axis=0, concat_axis=0, tiled=True)  14.9 us
  transfers between devices with their start and end apart: 1, of which 1 were waited for; matrix products, arithmetic and copies ran while one was open for 0% of the time, Pallas kernels for 0%

profile of v1, /device:TPU:1, one launch (start us, length us, event | category | flops | bytes accessed | tf_op | source)
XLA Modules:
  0.0 696.4 jit_solution(6827613463282353877)
XLA Ops:
  0.6 0.0 copy-start
  0.6 0.8 slice.125
  1.4 0.7 slice.126
  2.2 11.1 %tile.20 = bf16[2,2048,4095]{2,1,0:T(8,128)(2,1)} broadcast(bf16[2,4095]{1,0:T(2,128)(2,1)S(1)} %pad_maximum_fusion.3), dimensions={0,2} | broadcast | bytes 33562620 | tf_op jit(solution)/shard_map/tile | solution.py:30
  13.2 69.4 %reshape.275 = bf16[16773120]{0:T(1024)(128)(2,1)} reshape(bf16[2,2048,4095]{2,1,0:T(8,128)(2,1)} %tile.20) | data formatting | bytes 67092480
  82.6 39.9 %tile.21 = bf16[2,8386560]{1,0:T(2,128)(2,1)} reshape(bf16[16773120]{0:T(1024)(128)(2,1)} %reshape.275) | data formatting | bytes 67092480 | tf_op jit(solution)/shard_map/tile | solution.py:30
  122.6 27.0 %slice.127 = bf16[2,8384512]{1,0:T(2,128)(2,1)} slice(bf16[2,8386560]{1,0:T(2,128)(2,1)} %tile.21), slice={[0:2], [0:8384512]} | slice | bytes 67076096 | tf_op jit(solution)/shard_map/slice | solution.py:30
  149.6 52.8 %reshape.277 = bf16[16769024]{0:T(1024)(128)(2,1)} reshape(bf16[2,8384512]{1,0:T(2,128)(2,1)} %slice.127) | data formatting | bytes 67076096
  202.4 0.0 copy-start.1
  202.4 53.1 %reshape.273 = bf16[2,2048,4094]{2,1,0:T(8,128)(2,1)} reshape(bf16[16769024]{0:T(1024)(128)(2,1)} %reshape.277) | data formatting | bytes 67076096 | tf_op jit(solution)/shard_map/reshape | solution.py:31
  255.5 0.0 copy-done.1
  255.5 0.1 convert_element_type.35
  255.6 4.9 fusion
  260.5 4.9 fusion.1
  265.5 5.0 fusion.13
  270.4 5.0 fusion.12
  275.4 0.1 pad_maximum_fusion.1
  275.5 6.0 stack.19
  281.5 13.0 %all-to-all-start = ((bf16[32,1,2,64,2048]{4,3,2,1,0:T(8,128)(2,1)}), bf16[32,1,2,64,2048]{4,3,2,1,0:T(8,128)(2,1)}, u32[]{:S(2)}, u32[]{:S(2)}) async-start(bf16[32,1,2,64,2048]{4,3,2,1,0:T(8,128)(2,1)} %stack.19), calls=%async_computation | async-start | bytes 33554432 | tf_op jit(solution)/shard_map/all_to_all | solution.py:59
  294.5 0.0 copy-done
  294.5 0.1 dynamic-slice_bitcast_fusion
  294.6 0.1 slice.120
  294.7 0.9 tile.9
  295.7 0.4 slice.122
  296.1 1.5 reshape.272
  297.6 362.5 %all-to-all-done = bf16[32,1,2,64,2048]{4,3,2,1,0:T(8,128)(2,1)} async-done(((bf16[32,1,2,64,2048]{4,3,2,1,0:T(8,128)(2,1)}), bf16[32,1,2,64,2048]{4,3,2,1,0:T(8,128)(2,1)}, u32[]{:S(2)}, u32[]{:S(2)}) %all-to-all-start) | async-done | bytes 16777248 | tf_op jit(solution)/shard_map/all_to_all | solution.py:59
  660.2 7.0 fusion.17
  667.1 1.6 fusion.15
  668.7 1.6 fusion.14
  670.4 1.6 fusion.11
  672.0 1.6 fusion.10
  673.6 0.9 fusion.16
  674.5 0.9 add_reduce_fusion.1
  675.5 2.0 pad_maximum_fusion.5
  677.5 14.9 %all_to_all.11 = f32[32,1,3]{2,1,0:T(1,128)S(1)} all-to-all(f32[32,1,3]{2,1,0:T(1,128)S(1)} %broadcast_in_dim.2), channel_id=1, replica_groups=mesh['freq'=8,'panel'=32] {'panel'}, dimensions={0} | all-to-all | bytes 768 | tf_op jit(solution)/shard_map/all_to_all | solution.py:9
  692.3 0.1 reduce_sum.48
  692.4 0.7 fusion.18
  695.0 0.2 subtract_subtract_fusion
  695.1 1.0 pad_maximum_fusion
  (5 shorter events, 0.1 us)
Async XLA Ops:
  0.6 293.8 %copy-start = (bf16[1,2,4095]{2,1,0:T(2,128)(2,1)S(1)}, bf16[1,2,4095]{2,1,0:T(2,128)(2,1)}, u32[]{:S(2)}) copy-start(bf16[1,2,4095]{2,1,0:T(2,128)(2,1)} %param.5) | copy-start | bytes 49144
  202.4 53.1 %copy-start.1 = (f32[1,2,64,2048]{3,2,1,0:T(8,128)S(1)}, f32[1,2,64,2048]{3,2,1,0:T(8,128)}, u32[]{:S(2)}) copy-start(f32[1,2,64,2048]{3,2,1,0:T(8,128)} %param.3) | copy-start | bytes 3145732
  281.5 378.7 %all-to-all-start = ((bf16[32,1,2,64,2048]{4,3,2,1,0:T(8,128)(2,1)}), bf16[32,1,2,64,2048]{4,3,2,1,0:T(8,128)(2,1)}, u32[]{:S(2)}, u32[]{:S(2)}) async-start(bf16[32,1,2,64,2048]{4,3,2,1,0:T(8,128)(2,1)} %stack.19), calls=%async_computation | async-start | bytes 33554432 | tf_op jit(solution)/shard_map/all_to_all | solution.py:59
